TPU v7x, 32 devices: a whole 2x2x4 slice. The times are simulated.
32 devices in a mesh: data: 4 (over x, y), stage: 8 (over z, core).
Axes of the slice: x: 2, y: 2, z: 4, core: 2. Of those that a mesh axis runs over, the one named last changes fastest.
Arguments:
- hidden: bfloat16 [8, 1024, 2048], P('data', 'stage'), parts along dimension 0
- w_head: bfloat16 [32000, 2048], P('stage')
- labels: int32 [8, 1024], P('data'), parts along dimension 0
- loss_mask: int32 [8, 1024], P('data'), parts along dimension 0
- w_embed: bfloat16 [32000, 2048], P('stage')
- tok_ids: int32 [4096], P('data'), parts along dimension 0
- act_in: bfloat16 [32, 1024, 2048], P(('data', 'stage')), parts along dimension 0
- w_up: bfloat16 [8, 2048, 5632], P('stage')
- w_down: bfloat16 [8, 5632, 2048], P('stage')
Outputs:
- output 1: float32 [8], P('data'), parts along dimension 0
- output 2: float32 [8, 1024, 2048], P('data', 'stage'), parts along dimension 0
- output 3: bfloat16 [128000, 2048], P(('data', 'stage')), parts along dimension 0
- output 4: bfloat16 [4096, 2048], P(('data', 'stage')), parts along dimension 0
- output 5: bfloat16 [32, 1024, 2048], P(('data', 'stage')), parts along dimension 0
There are 4 independent parts. A program takes and returns all parts, laid end to end along the dimension named above; an argument that names none is the same for every part.
All inputs are finite; a program needn't handle non-finite values.
Results may differ from a plain program's by a relative error of at most 0.001.
Values are sent between devices in bfloat16 or wider.
A program may use at most 1 GiB of HBM per device.

v0:
```python
import jax
import jax.numpy as jnp
from jax import lax
from jax.sharding import PartitionSpec as P


def stage_body(hidden, w_head, labels, loss_mask, w_embed, tok_ids, act_in, w_up, w_down):
    stage_idx = lax.axis_index("stage")
    shard_rows = w_head.shape[0]
    start = stage_idx * shard_rows
    full_x = lax.all_gather(hidden, "stage", axis=1, tiled=True)
    micro_count, tokens, width = full_x.shape
    flat_x = full_x.reshape(micro_count * tokens, width)
    label_off = labels.reshape(micro_count * tokens) - start
    logits = lax.dot_general(flat_x, w_head, (((1,), (1,)), ((), ())), preferred_element_type=jnp.float32)
    is_label = lax.broadcasted_iota(jnp.int32, (1, shard_rows), 1) == label_off[:, None]
    peak = jnp.max(logits, axis=1)
    mass = jnp.sum(jnp.exp(logits - peak[:, None]), axis=1)
    picked = jnp.sum(jnp.where(is_label, logits, 0.0), axis=1)
    top_logit = lax.pmax(peak, "stage")
    norm_sum = lax.psum(mass * jnp.exp(peak - top_logit), "stage")
    target = lax.psum(picked, "stage")
    weights = loss_mask.astype(jnp.float32)
    kept_count = jnp.maximum(1.0, jnp.sum(weights, axis=1))
    per_token = (jnp.log(norm_sum) + top_logit - target).reshape(micro_count, tokens)
    micro_loss = jnp.sum(weights * per_token, axis=1) / kept_count
    tok_scale = (weights / kept_count[:, None]).reshape(micro_count * tokens)
    soft_probs = jnp.exp(logits - top_logit[:, None]) / norm_sum[:, None]
    grad_logits = ((soft_probs - is_label.astype(jnp.float32)) * tok_scale[:, None]).astype(jnp.bfloat16)
    part_dx = jnp.dot(grad_logits, w_head, preferred_element_type=jnp.float32).reshape(micro_count, tokens, width)
    grad_x = lax.psum_scatter(part_dx, "stage", scatter_dimension=1, tiled=True)
    grad_head = lax.dot_general(grad_logits, flat_x, (((0,), (0,)), ((), ())), preferred_element_type=jnp.float32).astype(jnp.bfloat16)
    id_off = tok_ids - start
    inside = (id_off >= 0) & (id_off < shard_rows)
    own_rows = jnp.take(w_embed, jnp.clip(id_off, 0, shard_rows - 1), axis=0)
    own_rows = jnp.where(inside[:, None], own_rows, jnp.zeros_like(own_rows))
    embedded = lax.psum_scatter(own_rows, "stage", scatter_dimension=0, tiled=True)
    layer_in = act_in[0]
    inner = jax.nn.gelu(jnp.dot(layer_in, w_up[0], preferred_element_type=jnp.float32), approximate=True).astype(jnp.bfloat16)
    mlp_out = (layer_in.astype(jnp.float32) + jnp.dot(inner, w_down[0], preferred_element_type=jnp.float32)).astype(jnp.bfloat16)
    return micro_loss, grad_x, grad_head, embedded, mlp_out[None]


def solution(mesh):
    by_rows = P(("data", "stage"), None)
    by_layer = P(("data", "stage"), None, None)
    return jax.shard_map(stage_body, mesh=mesh, in_specs=(P("data", "stage", None), P("stage", None), P("data", None), P("data", None), P("stage", None), P("data"), by_layer, P("stage", None, None), P("stage", None, None)), out_specs=(P("data"), P("data", "stage", None), by_rows, by_rows, by_layer), check_vma=False)
```

profile of v0, /device:TPU:0, one launch (start us, length us, event | category | flops | bytes accessed | tf_op | source)
XLA Modules:
  0.0 429.9 jit_solution(6710385684524579866)
XLA Ops:
  7.2 0.0 all-gather.2.cloned.1.call-start
  7.2 0.7 all-gather.2.cloned.1.call-update
  7.9 0.0 reduce-scatter.5.cloned.1.call-start
  8.0 0.7 fusion.29
  8.6 0.0 copy-start.1
  8.7 0.0 copy-start.2
  8.7 16.6 %gather_fusion = bf16[1024,2048]{1,0:T(8,128)(2,1)} fusion(bf16[4000,2048]{1,0:T(8,128)(2,1)} %param.13, s32[1024]{0:T(1024)S(1)} %fusion.29), kind=kCustom, calls=%fused_computation | custom fusion | bytes 8392704 | tf_op jit(solution)/shard_map/jit(_take)/gather | solution.py:35
  25.3 0.0 copy-done.1
  25.3 4.1 select_select_fusion
  29.3 0.0 reduce-scatter.5.cloned.1.call-update
  29.4 0.0 reduce-scatter.3.cloned.1.call-start
  29.4 0.0 copy-done.2
  29.5 64.4 %all-gather.2.cloned.1.call-done = bf16[2,1024,2048]{2,1,0:T(8,128)(2,1)} async-done(((bf16[2,128,2048]{2,1,0:T(8,128)(2,1)}), bf16[2,1024,2048]{2,1,0:T(8,128)(2,1)}) %all-gather.2.cloned.1.call-update) | async-done | bytes 8388624 | tf_op jit(solution)/shard_map/all_gather | solution.py:11
  93.8 42.0 %fusion.35 = (f32[2048]{0:T(1024)S(1)}, f32[2048,4000]{0,1:T(8,128)}) fusion(bf16[2048,2048]{1,0:T(8,128)(2,1)} %bitcast.57, bf16[4000,2048]{1,0:T(8,128)(2,1)} %param.10), kind=kOutput, calls=%fused_computation.45 | convolution fusion | flops 33562621952 | bytes 57548800 | tf_op jit(solution)/shard_map/dot_general | solution.py:15
  135.8 15.3 %pmax.7 = f32[2048]{0:T(1024)S(1)} all-reduce(f32[2048]{0:T(1024)S(1)} %get-tuple-element.15), channel_id=1, replica_groups=mesh['data'=4,'stage'=8] {'stage'}, use_global_device_ids=true, to_apply=%region_2.3 | all-reduce | flops 2048 | bytes 16384 | tf_op jit(solution)/shard_map/pmax | solution.py:20
  151.1 0.0 copy-start
  151.1 14.8 %exponential_reduce_fusion = (f32[2048]{0:T(1024)S(1)}, f32[2048]{0:T(1024)S(1)}) fusion(f32[2048,4000]{0,1:T(8,128)} %get-tuple-element.16, f32[2048]{0:T(1024)S(1)} %get-tuple-element.15, s32[2048]{0:T(1024)S(1)} %bitcast.54), kind=kLoop, calls=%fused_computation.5 | loop fusion | flops 40955904 | bytes 32800768 | tf_op jit(solution)/shard_map/reduce_sum | solution.py:18
  165.9 26.1 %all-reduce = (f32[2048]{0:T(1024)S(1)}, f32[2048]{0:T(1024)S(1)}) all-reduce(f32[2048]{0:T(1024)S(1)} %get-tuple-element.6, f32[2048]{0:T(1024)S(1)} %exponential_multiply_fusion), channel_id=1, replica_groups=mesh['data'=4,'stage'=8] {'stage'}, use_global_device_ids=true, to_apply=%region_5.6 | all-reduce | flops 4096 | bytes 32768 | tf_op jit(solution)/shard_map/psum | solution.py:22
  192.1 0.0 copy-done
  192.1 0.2 convert_reduce_fusion
  192.2 0.5 broadcast_maximum_fusion
  192.8 0.1 divide_bitcast_fusion
  192.8 20.7 %multiply_convert_fusion = bf16[2048,4000]{0,1:T(8,128)(2,1)} fusion(f32[2048,4000]{0,1:T(8,128)} %get-tuple-element.16, f32[2048]{0:T(1024)S(1)} %bitcast.56, f32[2048]{0:T(1024)S(1)} %get-tuple-element.10, f32[2048]{0:T(1024)S(1)} %pmax.7, s32[2048]{0:T(1024)S(1)} %bitcast.55), kind=kLoop, calls=%fused_computation.2 | loop fusion | flops 57344000 | bytes 49184768 | tf_op jit(solution)/shard_map/convert_element_type | solution.py:29
  213.6 43.5 %fusion.36 = f32[2048,2048]{1,0:T(8,128)} fusion(bf16[2048,4000]{0,1:T(8,128)(2,1)} %multiply_convert_fusion, bf16[4000,2048]{1,0:T(8,128)(2,1)} %param.10), kind=kOutput, calls=%fused_computation.46 | convolution fusion | flops 33554432000 | bytes 49545216 | tf_op jit(solution)/shard_map/dot_general | solution.py:30
  257.1 0.0 reduce-scatter.3.cloned.1.call-update
  257.1 0.0 copy-start.3
  257.1 0.0 slice-start
  257.1 0.0 slice-start.1
  257.2 0.0 slice-start.2
  257.2 36.8 %fusion.7.clone.6 = bf16[1024,5632]{1,0:T(8,128)(2,1)} fusion(bf16[1,2048,5632]{2,1,0:T(8,128)(2,1)} %param.16, bf16[1,1024,2048]{2,1,0:T(8,128)(2,1)} %param.15), kind=kOutput, calls=%fused_computation.13.clone.clone.clone.clone.clone.1 | convolution fusion | flops 23674224640 | bytes 38797312 | tf_op jit(solution)/shard_map/dot_general | solution.py:39
  293.9 0.0 copy-done.3
  293.9 0.0 slice-start.3
  293.9 31.7 %fusion.20 = bf16[1,1024,2048]{2,1,0:T(8,128)(2,1)} fusion(bf16[1,1024,2048]{2,1,0:T(8,128)(2,1)S(1)} %copy-done.3, bf16[1,5632,2048]{2,1,0:T(8,128)(2,1)} %param.17, bf16[1024,5632]{1,0:T(8,128)(2,1)} %fusion.7.clone.6), kind=kOutput, calls=%fused_computation.24 | convolution fusion | flops 23628611584 | bytes 42991616 | tf_op jit(solution)/shard_map/dot_general | solution.py:40
  325.6 0.0 slice-done
  325.6 0.0 slice-done.1
  325.6 0.0 slice-done.2
  325.6 0.0 slice-done.3
  325.6 40.7 %convolution_convert_fusion = bf16[4000,2048]{1,0:T(8,128)(2,1)} fusion(bf16[2048,4000]{0,1:T(8,128)(2,1)S(1)} %bitcast.53, bf16[2048,2048]{1,0:T(8,128)(2,1)} %bitcast.58), kind=kOutput, calls=%fused_computation.18 | convolution fusion | flops 33562624000 | bytes 41156608 | tf_op jit(solution)/shard_map/dot_general | solution.py:32
  366.4 0.0 reduce-scatter.5.cloned.1.call-done
  366.4 57.0 %reduce-scatter.3.cloned.1.call-done = f32[2,128,2048]{2,1,0:T(8,128)} async-done(((f32[2,1024,2048]{2,1,0:T(8,128)}), f32[2,128,2048]{2,1,0:T(8,128)}) %reduce-scatter.3.cloned.1.call-update) | async-done | bytes 2097168 | tf_op jit(solution)/shard_map/reduce_scatter | solution.py:31
  (8 shorter events, 0.1 us)
Async XLA Ops:
  7.2 86.7 %all-gather.2.cloned.1.call-start = ((), (), s32[]{:S(2)}) async-start(), calls=%async_computation.2 | async-start | bytes 9437184 | tf_op jit(solution)/shard_map/all_gather | solution.py:11
  7.9 358.5 %reduce-scatter.5.cloned.1.call-start = ((), (), s32[]{:S(2)}) async-start(), calls=%async_computation.4 | async-start | bytes 4718592 | tf_op jit(solution)/shard_map/reduce_scatter | solution.py:37
  8.6 16.6 %copy-start.1 = (s32[1024]{0:T(1024)S(1)}, s32[1024]{0:T(1024)}, u32[]{:S(2)}) copy-start(s32[1024]{0:T(1024)} %param.14) | copy-start | bytes 12292
  8.7 20.8 %copy-start.2 = (s32[2,1024]{1,0:T(2,128)S(1)}, s32[2,1024]{1,0:T(2,128)}, u32[]{:S(2)}) copy-start(s32[2,1024]{1,0:T(2,128)} %param.11) | copy-start | bytes 24580
  29.4 394.0 %reduce-scatter.3.cloned.1.call-start = ((), (), s32[]{:S(2)}) async-start(), calls=%async_computation.3 | async-start | bytes 18874368 | tf_op jit(solution)/shard_map/reduce_scatter | solution.py:31
  151.1 41.0 %copy-start = (s32[2,1024]{1,0:T(2,128)S(1)}, s32[2,1024]{1,0:T(2,128)}, u32[]{:S(2)}) copy-start(s32[2,1024]{1,0:T(2,128)} %param.12) | copy-start | bytes 24580
  257.1 36.8 %copy-start.3 = (bf16[1,1024,2048]{2,1,0:T(8,128)(2,1)S(1)}, bf16[1,1024,2048]{2,1,0:T(8,128)(2,1)}, u32[]{:S(2)}) copy-start(bf16[1,1024,2048]{2,1,0:T(8,128)(2,1)} %param.15) | copy-start | bytes 12582916
  257.1 68.5 %slice-start = ((s8[16384000]{0:T(1024)(128)(4,1)}), s8[4194304]{0:T(1024)(128)(4,1)S(1)}, s32[]{:S(2)}) async-start(s8[16384000]{0:T(1024)(128)(4,1)} %bitcast.52), calls=%async_computation.5 | async-start | bytes 8388608
  257.1 68.5 %slice-start.1 = ((s8[16384000]{0:T(1024)(128)(4,1)}), s8[4194304]{0:T(1024)(128)(4,1)S(1)}, s32[]{:S(2)}) async-start(s8[16384000]{0:T(1024)(128)(4,1)} %bitcast.52), calls=%async_computation.6 | async-start | bytes 8388608
  257.2 68.5 %slice-start.2 = ((s8[16384000]{0:T(1024)(128)(4,1)}), s8[4194304]{0:T(1024)(128)(4,1)S(1)}, s32[]{:S(2)}) async-start(s8[16384000]{0:T(1024)(128)(4,1)} %bitcast.52), calls=%async_computation.7 | async-start | bytes 8388608
  293.9 31.7 %slice-start.3 = ((s8[16384000]{0:T(1024)(128)(4,1)}), s8[3801088]{0:T(1024)(128)(4,1)S(1)}, s32[]{:S(2)}) async-start(s8[16384000]{0:T(1024)(128)(4,1)} %bitcast.52), calls=%async_computation.8 | async-start | bytes 7602176
Sparse Core Ops, SparseCore 0:
  9.6 84.1 all-gather.1
  96.7 48.8 reduce-scatter.4
  257.2 166.0 reduce-scatter.2
where the time goes:
time: 430 us
  matrix products  195 us (45%)
  waiting for transfers between devices  122 us (28%)
  blocking collectives  41.4 us (10%)
  other arithmetic  41.1 us (10%)
  local copies, waits for them, and re-layouts  16.7 us (4%)
  between operations  13.9 us (3%)
    all_gather x1, waiting for transfers between devices, stage_body(): full_x = lax.all_gather(hidden, 'stage', axis=1, tiled=True)  64.4 us
    reduce_scatter x1, waiting for transfers between devices, stage_body(): grad_x = lax.psum_scatter(part_dx, 'stage', scatter_dimension=1, tiled=True)  57 us
    dot_general x1, matrix products, stage_body(): jnp.dot(grad_logits, w_head, preferred_element_type=jnp.float32)  43.5 us
    dot_general x1, matrix products, stage_body(): lax.dot_general(flat_x, w_head, (((1,), (1,)), ((), ())), preferred_eleme...  42 us
    dot_general x1, matrix products, stage_body(): lax.dot_general(grad_logits, flat_x, (((0,), (0,)), ((), ())), preferred_...  40.7 us
    dot_general x1, matrix products, stage_body(): jnp.dot(layer_in, w_up[0], preferred_element_type=jnp.float32)  36.8 us
    dot_general x1, matrix products, stage_body(): jnp.dot(inner, w_down[0], preferred_element_type=jnp.float32)  31.7 us
    psum x1, blocking collectives, stage_body(): target = lax.psum(picked, 'stage')  26.1 us
  transfers between devices with their start and end apart: 3, of which 2 were waited for; matrix products, arithmetic and copies ran while one was open for 59% of the time, Pallas kernels for 0%

commit v1 on v0

v1 whole, which is shorter than its diff:
```python
import functools

import jax
import jax.numpy as jnp
from jax import lax
from jax.experimental import pallas as pl
from jax.experimental.pallas import tpu as pltpu
from jax.sharding import PartitionSpec as P

MESH = pl.DeviceIdType.MESH
F32, BF16 = jnp.float32, jnp.bfloat16
LANES = 128


def chunks_of(total, size):
    return [(a, min(size, total - a)) for a in range(0, total, size)]


def nt_dot(a, b):
    return lax.dot_general(a, b, (((1,), (1,)), ((), ())), preferred_element_type=F32)


def head_kernel(n, tile, chunk, x0_hbm, hid_ref, rows_ref, w_hbm, g_hbm, xall, dx0_hbm, dx1_hbm, prx, prx1, rx, lse_ref, tgt_ref,
                w, z, xbuf, cols, g_buf, blk, dxb, stage, mine, peers,
                w_sem, x_sem, xs_sem, own_sem, ag_send, ag_recv, st_send, st_recv, g_sem,
                pr_send, pr_recv, pr1_send, pr1_recv, rs_send, rs_recv, stage_sem, out_sem, out1_sem):
    me = lax.axis_index("stage")
    zc, c = me // 2, me % 2
    inner_to_outer = 3 * zc - 3
    other_inner = 3 - zc
    outer_to_inner = zc + 1 - 2 * (zc // 2)
    is_outer = (zc == 0) | (zc == 3)
    is_inner = (zc == 1) | (zc == 2)
    my_outer = 3 * (zc // 2)
    other_outer = 3 - my_outer
    tokens = x0_hbm.shape[0]
    rows = w_hbm.shape[0]
    steps = tokens // tile
    half = tile // 2
    parts = chunks_of(rows, chunk)
    own_half = pl.ds(pl.multiple_of(c * half, half), half)
    peer_half = pl.ds(pl.multiple_of((1 - c) * half, half), half)

    def remote(src, dst, ss, rs, tz, tc):
        return pltpu.make_async_remote_copy(src, dst, ss, rs, device_id={"stage": tz * 2 + tc}, device_id_type=MESH)

    loads = [pltpu.make_async_copy(w_hbm.at[pl.ds(a, s)], w.at[pl.ds(a, s)], w_sem.at[i]) for i, (a, s) in enumerate(parts)]

    def x_load(j, i, slot):
        at = pl.multiple_of(i * tile, tile)
        src = x0_hbm.at[pl.ds(at, tile)] if j == 0 else xall.at[pl.ds(pl.multiple_of(tokens + at, tile), tile)]
        return pltpu.make_async_copy(src, xbuf.at[slot], x_sem.at[slot])

    def x_store(i, slot):
        return pltpu.make_async_copy(xbuf.at[slot], xall.at[pl.ds(pl.multiple_of(i * tile, tile), tile)], xs_sem.at[slot])

    def xrows(tz, tc):
        return xall.at[pl.ds(pl.multiple_of(tokens + (tz * 2 + tc) * half, half), half)]

    x_load(0, 0, 0).start()
    for load in loads:
        load.start()
    barrier = pltpu.get_barrier_semaphore()
    for k in range(1, n):
        pl.semaphore_signal(barrier, inc=1, device_id={"stage": lax.rem(me + k, n)}, device_id_type=MESH)

    def set_cols(j, lse):
        sub = lax.broadcasted_iota(jnp.int32, (LANES, LANES), 0)
        for i in range(tokens // LANES):
            seg = slice(i * LANES, (i + 1) * LANES)
            tall = jnp.where(sub == 0, rows_ref[j, 0:1, seg], rows_ref[j, 1:2, seg])
            if lse is not None:
                tall = jnp.where(sub == 2, lse[:, seg], tall)
            cols[pl.ds(i * LANES, LANES), :] = tall.T

    def logits_tile(j, i, slot, first):
        at = pl.multiple_of(i * tile, tile)
        off = cols[pl.ds(at, tile), 0:1].astype(jnp.int32)
        x = xbuf[slot]
        run = None

        def fold(run, zp, a, s):
            top = jnp.max(zp, axis=1, keepdims=True)
            hit = lax.broadcasted_iota(jnp.int32, (1, s), 1) == off - a
            hits = jnp.sum(jnp.where(hit, zp, 0.0), axis=1, keepdims=True)
            if run is None:
                return top, jnp.sum(jnp.exp(zp - top), axis=1, keepdims=True), hits
            peak, mass, picked = run
            new = jnp.maximum(peak, top)
            mass = mass * jnp.exp(peak - new) + jnp.sum(jnp.exp(zp - new), axis=1, keepdims=True)
            return new, mass, picked + hits

        held = None
        for k, (a, s) in enumerate(parts):
            if first:
                loads[k].wait()
            zp = nt_dot(x, w[pl.ds(a, s), :])
            z[pl.ds(at, tile), pl.ds(a, s)] = zp
            if held is not None:
                run = fold(run, *held)
            held = (zp, a, s)
        peak, mass, picked = fold(run, *held)
        lane = lax.broadcasted_iota(jnp.int32, (tile, LANES), 1)
        packed = jnp.where(lane == 0, peak, jnp.where(lane == 1, mass, picked))
        mine[j, :, pl.ds(at, tile)] = packed.T[:8, :]

    def stat_copy(j, k):
        return pltpu.make_async_remote_copy(
            mine.at[j], peers.at[j, k], st_send.at[j, k], st_recv.at[j, k],
            device_id={"stage": lax.rem(me + k, n)}, device_id_type=MESH)

    def stat_send(j):
        for k in range(1, n):
            stat_copy(j, k).start()

    def stat_finish(j):
        for k in range(1, n):
            stat_copy(j, k).wait()
        stats = [mine[j]] + [peers[j, k] for k in range(1, n)]
        top = functools.reduce(jnp.maximum, [s[0:1] for s in stats])
        lse = top + jnp.log(sum(s[1:2] * jnp.exp(s[0:1] - top) for s in stats))
        lse_ref[j] = lse
        tgt_ref[j] = sum(s[2:3] for s in stats)
        set_cols(j, lse)

    def g_copy(j, at, slot):
        return pltpu.make_async_copy(g_buf.at[slot], g_hbm.at[pl.ds(pl.multiple_of(j * tokens + at, tile), tile)], g_sem.at[slot])

    def grad_tile(j, at, slot):
        off = cols[pl.ds(at, tile), 0:1].astype(jnp.int32)
        scale = cols[pl.ds(at, tile), 1:2]
        base = cols[pl.ds(at, tile), 2:3]
        def grad_part(a, s):
            soft = jnp.exp(z[pl.ds(at, tile), pl.ds(a, s)] - base)
            hit = lax.broadcasted_iota(jnp.int32, (1, s), 1) == off - a
            g = ((soft - jnp.where(hit, 1.0, 0.0)) * scale).astype(BF16)
            g_buf[slot, :, pl.ds(a, s)] = g
            return g

        acc = None
        g = grad_part(*parts[0])
        for k, (a, s) in enumerate(parts):
            ahead = grad_part(*parts[k + 1]) if k + 1 < len(parts) else None
            part = jnp.dot(g, w[pl.ds(a, s), :], preferred_element_type=F32)
            acc = part if acc is None else acc + part
            g = ahead
        return acc

    def pair_copy(s):
        return remote(blk.at[s, peer_half], prx.at[s], pr_send.at[s], pr_recv.at[s], zc, 1 - c)

    def rs_copy(s, k, tz):
        return remote(blk.at[s, own_half], rx.at[k], rs_send.at[k], rs_recv.at[k], tz, c)

    def combine(s, slots):
        pair_copy(s).wait_recv()
        stages = [pltpu.make_async_copy(prx.at[s], stage.at[0], stage_sem.at[0])]
        stages[0].start()
        for q, k in enumerate(slots):
            rs_copy(s, k, zc).wait_recv()
            copy = pltpu.make_async_copy(rx.at[k], stage.at[1 + q], stage_sem.at[1 + q])
            copy.start()
            stages.append(copy)
        for copy in stages:
            copy.wait()

        @pl.loop(0, half // 16)
        def _(r):
            here = pl.ds(pl.multiple_of(c * half + r * 16, 16), 16)
            there = pl.ds(pl.multiple_of(r * 16, 16), 16)
            total = blk[s, here, :] + stage[0, there, :]
            for q in range(len(slots)):
                total = total + stage[1 + q, there, :]
            blk[s, here, :] = total

    set_cols(0, None)
    pl.semaphore_wait(barrier, n - 1)
    own = pltpu.make_async_copy(hid_ref, xrows(zc, c), own_sem)
    own.start()

    def ag(src, block, snd, rcv, tz, tc, bc):
        return remote(src, xrows(block, bc), ag_send.at[snd], ag_recv.at[rcv], tz, tc)

    def to_partner():
        return ag(hid_ref, zc, 0, 0, zc, 1 - c, c)

    to_partner().start()

    def hop_outer():
        return ag(hid_ref, zc, 1, 1, outer_to_inner, c, c)

    def hop_inner(i):
        if i == 0:
            return ag(hid_ref, zc, 1, 1, inner_to_outer, c, c)
        if i == 1:
            return ag(hid_ref, zc, 2, 2, other_inner, c, c)
        if i == 2:
            return ag(xrows(my_outer, c), my_outer, 3, 3, other_inner, c, c)
        if i == 3:
            return ag(xrows(other_inner, c), other_inner, 4, 2, inner_to_outer, c, c)
        return ag(xrows(other_outer, c), other_outer, 5, 3, inner_to_outer, c, c)

    def got(block, rcv, bc):
        ag(hid_ref, block, 0, rcv, zc, c, bc).wait_recv()

    def forward(k):
        block = lax.rem(zc + k, 4)
        return ag(xrows(block, c), block, 5 + k, 3 + k, zc, 1 - c, c)

    @pl.when(is_outer)
    def _():
        hop_outer().start()

    @pl.when(is_inner)
    def _():
        hop_inner(0).start()
        hop_inner(1).start()

    x_load(0, 0, 0).wait()
    x_load(0, 1, 1).start()
    x_store(0, 0).start()
    logits_tile(0, 0, 0, True)

    @pl.loop(1, steps)
    def _(i):
        slot = lax.rem(i, 2)
        x_load(0, i, slot).wait()
        x_store(i - 1, 1 - slot).wait()

        @pl.when(i < steps - 1)
        def _():
            x_load(0, i + 1, 1 - slot).start()

        x_store(i, slot).start()
        logits_tile(0, i, slot, False)

        @pl.when((i == 1) & is_inner)
        def _():
            got(my_outer, 1, c)
            hop_inner(2).start()
            got(other_inner, 2, c)
            hop_inner(3).start()

    x_store(steps - 1, (steps - 1) % 2).wait()
    stat_send(0)

    @pl.when(is_inner)
    def _():
        got(other_outer, 3, c)
        hop_inner(4).start()

    stat_finish(0)

    @pl.loop(0, steps)
    def _(s):
        slot = lax.rem(s, 2)
        far = zc // 2
        pick = jnp.where(s == 0, 3 - 3 * far, jnp.where(s == 1, 2 - far, jnp.where(s == 2, zc + 1 - 2 * (zc % 2), zc)))
        at = pl.multiple_of(pick * tile, tile)

        @pl.when(s >= 2)
        def _():
            g_copy(0, 0, slot).wait()

        blk[s] = grad_tile(0, at, slot)
        g_copy(0, at, slot).start()
        pair_copy(s).start()

        @pl.when((s == 1) & is_outer)
        def _():
            combine(0, [])
            rs_copy(0, 0, outer_to_inner).start()

        @pl.when(s == 2)
        def _():
            @pl.when(is_outer)
            def _():
                got(outer_to_inner, 1, c)
                got(3 - outer_to_inner, 2, c)
                got(other_outer, 3, c)
            for k in (1, 2, 3):
                forward(k).start()

    for slot in range(2):
        g_copy(0, 0, slot).wait()
    got(zc, 0, 1 - c)
    own.wait()
    for k in (1, 2, 3):
        got(lax.rem(zc + k, 4), 3 + k, 1 - c)

    set_cols(1, None)
    x_load(1, 0, 0).start()

    @pl.loop(0, steps)
    def _(i):
        slot = lax.rem(i, 2)
        x_load(1, i, slot).wait()

        @pl.when(i < steps - 1)
        def _():
            x_load(1, i + 1, 1 - slot).start()

        logits_tile(1, i, slot, False)

        @pl.when((i == 0) & is_outer)
        def _():
            combine(1, [])
            rs_copy(1, 1, outer_to_inner).start()

        @pl.when((i == 1) & is_inner)
        def _():
            combine(0, [0])
            rs_copy(0, 3, other_inner).start()

    stat_send(1)

    @pl.when(is_outer)
    def _():
        combine(2, [])
        rs_copy(2, 2, outer_to_inner).start()

    stat_finish(1)

    def pair1(i, slot):
        return remote(dxb.at[slot, peer_half], prx1.at[i], pr1_send.at[slot], pr1_recv.at[i], zc, 1 - c)

    def out1(i, slot):
        return pltpu.make_async_copy(dxb.at[slot, own_half], dx1_hbm.at[i], out1_sem.at[slot])

    def finish1(i, slot):
        pair1(i, slot).wait_recv()
        copy = pltpu.make_async_copy(prx1.at[i], stage.at[0], stage_sem.at[0])
        copy.start()
        copy.wait()

        @pl.loop(0, half // 16)
        def _(r):
            here = pl.ds(pl.multiple_of(c * half + r * 16, 16), 16)
            dxb[slot, here, :] = dxb[slot, here, :] + stage[0, pl.ds(pl.multiple_of(r * 16, 16), 16), :]

        out1(i, slot).start()

    @pl.loop(0, steps)
    def _(i):
        slot = lax.rem(i, 2)

        @pl.when(i >= 2)
        def _():
            g_copy(1, 0, slot).wait()
            pair1(i - 2, slot).wait_send()
            out1(i - 2, slot).wait()

        dxb[slot] = grad_tile(1, pl.multiple_of(i * tile, tile), slot)
        g_copy(1, pl.multiple_of(i * tile, tile), slot).start()
        pair1(i, slot).start()

        @pl.when(i >= 1)
        def _():
            finish1(i - 1, 1 - slot)

        @pl.when((i == 0) & is_inner)
        def _():
            combine(1, [1])
            rs_copy(1, 4, other_inner).start()
            combine(2, [3])
            rs_copy(2, 5, inner_to_outer).start()

    finish1(steps - 1, (steps - 1) % 2)
    for i in range(steps - 2, steps):
        g_copy(1, 0, i % 2).wait()
        pair1(i, i % 2).wait_send()
        out1(i, i % 2).wait()

    @pl.when(is_outer)
    def _():
        combine(3, [5])

    @pl.when(is_inner)
    def _():
        combine(3, [2, 4])

    final = pltpu.make_async_copy(blk.at[3, own_half], dx0_hbm, out_sem)
    final.start()
    to_partner().wait_send()
    for k in (1, 2, 3):
        forward(k).wait_send()
    for s in range(steps):
        pair_copy(s).wait_send()

    @pl.when(is_outer)
    def _():
        hop_outer().wait_send()
        for k in range(3):
            rs_copy(k, k, outer_to_inner).wait_send()

    @pl.when(is_inner)
    def _():
        for i in range(5):
            hop_inner(i).wait_send()
        rs_copy(0, 3, other_inner).wait_send()
        rs_copy(1, 4, other_inner).wait_send()
        rs_copy(2, 5, inner_to_outer).wait_send()

    final.wait()


def head(x0, hid1, rows_in, w, n, tile=256, chunk=1024):
    tokens, width = x0.shape
    rows = w.shape[0]
    half = tile // 2
    steps = tokens // tile
    vmem = pl.BlockSpec(memory_space=pltpu.VMEM)
    hbm = pl.BlockSpec(memory_space=pl.ANY)
    nchunk = len(chunks_of(rows, chunk))
    dma = pltpu.SemaphoreType.DMA
    sds = jax.ShapeDtypeStruct
    return pl.pallas_call(
        functools.partial(head_kernel, n, tile, chunk),
        out_shape=(sds((2 * tokens, rows), BF16), sds((2 * tokens, width), BF16), sds((half, width), F32),
                   sds((steps, half, width), F32), sds((steps, half, width), F32), sds((steps, half, width), F32),
                   sds((6, half, width), F32), sds((2, 1, tokens), F32), sds((2, 1, tokens), F32)),
        in_specs=[hbm, vmem, vmem, hbm],
        out_specs=(hbm, hbm, hbm, hbm, hbm, hbm, hbm, vmem, vmem),
        scratch_shapes=[
            pltpu.VMEM((rows, width), BF16),
            pltpu.VMEM((tokens, rows), F32),
            pltpu.VMEM((2, tile, width), BF16),
            pltpu.VMEM((tokens, LANES), F32),
            pltpu.VMEM((2, tile, rows), BF16),
            pltpu.VMEM((steps, tile, width), F32),
            pltpu.VMEM((2, tile, width), F32),
            pltpu.VMEM((3, half, width), F32),
            pltpu.VMEM((2, 8, tokens), F32),
            pltpu.VMEM((2, n, 8, tokens), F32),
            dma((nchunk,)), dma((2,)), dma((2,)), dma,
            dma((9,)), dma((7,)), dma((2, n)), dma((2, n)), dma((2,)),
            dma((steps,)), dma((steps,)), dma((2,)), dma((steps,)), dma((6,)), dma((6,)), dma((3,)), dma, dma((2,)),
        ],
        compiler_params=pltpu.CompilerParams(collective_id=0, has_side_effects=True, vmem_limit_bytes=67043328),
        cost_estimate=pl.CostEstimate(flops=8 * tokens * rows * width, bytes_accessed=80_000_000, transcendentals=4 * tokens * rows),
        name="head",
    )(x0, hid1, rows_in, w)


def stage_body(hidden, w_head, labels, loss_mask, w_embed, tok_ids, act_in, w_up, w_down):
    n = 8
    stage_idx = lax.axis_index("stage")
    shard_rows = w_head.shape[0]
    start = stage_idx * shard_rows
    x0 = lax.all_gather(hidden[0], "stage", axis=0, tiled=True)
    weights = loss_mask.astype(F32)
    kept_count = jnp.maximum(1.0, jnp.sum(weights, axis=1))
    tok_scale = weights / kept_count[:, None]

    layer_in = act_in[0]
    inner = jax.nn.gelu(jnp.dot(layer_in, w_up[0], preferred_element_type=F32), approximate=True).astype(BF16)
    id_off = tok_ids - start
    inside = (id_off >= 0) & (id_off < shard_rows)
    own_rows = jnp.take(w_embed, jnp.clip(id_off, 0, shard_rows - 1), axis=0)
    own_rows = jnp.where(inside[:, None], own_rows, jnp.zeros_like(own_rows))

    embedded = lax.psum_scatter(own_rows, "stage", scatter_dimension=0, tiled=True)
    inner, own_rows, x0 = lax.optimization_barrier((inner, own_rows, x0))

    rows_in = jnp.stack([(labels - start).astype(F32), tok_scale], axis=1)
    g, x_all, dx0, dx1, _, _, _, lse, target = head(x0, hidden[1], rows_in, w_head, n)
    dx1, embedded = lax.optimization_barrier((dx1, embedded))
    dx1 = lax.psum_scatter(dx1, "stage", scatter_dimension=0, tiled=False, axis_index_groups=[[0, 2, 4, 6], [1, 3, 5, 7]])
    micro_loss = jnp.sum(weights * (lse[:, 0] - target[:, 0]), axis=1) / kept_count
    grad_head = lax.dot_general(g, x_all, (((0,), (0,)), ((), ())), preferred_element_type=F32).astype(BF16)
    mlp_out = (layer_in.astype(F32) + jnp.dot(inner, w_down[0], preferred_element_type=F32)).astype(BF16)
    return micro_loss, jnp.stack([dx0, dx1]), grad_head, embedded, mlp_out[None]


def solution(mesh):
    by_rows = P(("data", "stage"), None)
    by_layer = P(("data", "stage"), None, None)
    return jax.shard_map(stage_body, mesh=mesh, in_specs=(P("data", "stage", None), P("stage", None), P("data", None), P("data", None), P("stage", None), P("data"), by_layer, P("stage", None, None), P("stage", None, None)), out_specs=(P("data"), P("data", "stage", None), by_rows, by_rows, by_layer), check_vma=False)
```

time: 430 us -> 332 us (0.77)
  Pallas kernels: 0 us -> 173 us
  waiting for transfers between devices: 122 us -> 3.7 us
  matrix products: 195 us -> 108 us
  blocking collectives: 41.4 us -> 0 us
  other arithmetic: 41.1 us -> 9.01 us
    pallas_call x0 -> x1, Pallas kernels: none -> 173 us  [head(): pl.pallas_call(functools.partial(head_kernel, n, tile, chunk), out_shape=...]
    dot_general x5 -> x3, matrix products: 195 us -> 108 us  [the longest x1 41.2 us: stage_body(): lax.dot_general(g, x_all, (((0,), (0,)), ((), ())), preferred_element_typ...]
    all_gather x1, waiting for transfers between devices: 64.4 us -> 0.01 us  [stage_body(): x0 = lax.all_gather(hidden[0], 'stage', axis=0, tiled=True)]
    reduce_scatter x1, waiting for transfers between devices: 57 us -> 3.63 us  [stage_body(): lax.psum_scatter(dx1, 'stage', scatter_dimension=0, tiled=False, axis_ind...]
    psum x1 -> x0, blocking collectives: 26.1 us -> none  [stage_body(): target = lax.psum(picked, 'stage')]
    convert_element_type x1, other arithmetic: 20.7 us -> 0.01 us  [stage_body(): rows_in = jnp.stack([(labels - start).astype(F32), tok_scale], axis=1)]
    pmax x1 -> x0, blocking collectives: 15.3 us -> none  [stage_body(): top_logit = lax.pmax(peak, 'stage')]
    reduce_sum x1, other arithmetic: 14.8 us -> 0.12 us  [stage_body(): jnp.sum(weights * (lse[:, 0] - target[:, 0]), axis=1) / kept_count]
  transfers between devices with their start and end apart: 3 -> 3, of which waited for: 2 -> 1; matrix products, arithmetic and copies ran while one was open for 59% -> 40% of each run, Pallas kernels for 0% -> 53%
where the time goes in v1:
time: 332 us; the launch traced here: 328 us
  Pallas kernels  173 us (52%)
  matrix products  108 us (33%)
  local copies, waits for them, and re-layouts  19.4 us (6%)
  between operations  14.1 us (4%)
  other arithmetic  9.01 us (3%)
  waiting for transfers between devices  3.7 us (1%)
    pallas_call x1, Pallas kernels, head(): pl.pallas_call(functools.partial(head_kernel, n, tile, chunk), out_shape=...  173 us
    dot_general x1, matrix products, stage_body(): lax.dot_general(g, x_all, (((0,), (0,)), ((), ())), preferred_element_typ...  41.2 us
    dot_general x1, matrix products, stage_body(): jnp.dot(layer_in, w_up[0], preferred_element_type=F32)  35 us
    dot_general x1, matrix products, stage_body(): jnp.dot(inner, w_down[0], preferred_element_type=F32)  32.1 us
    gather x1, local copies, waits for them, and re-layouts, stage_body(): own_rows = jnp.take(w_embed, jnp.clip(id_off, 0, shard_rows - 1), axis=0)  16.6 us
  transfers between devices with their start and end apart: 3, of which 1 were waited for; matrix products, arithmetic and copies ran while one was open for 40% of the time, Pallas kernels for 53%

profile of v1, /device:TPU:0, one launch (start us, length us, event | category | flops | bytes accessed | tf_op | source)
XLA Modules:
  0.0 328.3 jit_solution(18343117574858611539)
XLA Ops:
  7.2 0.0 all-gather.3.cloned.1.call-start
  7.2 2.3 slice_bitcast_fusion
  9.5 0.0 all-gather.3.cloned.1.call-update
  9.5 0.0 reduce-scatter.3.cloned.1.call-start
  9.6 0.7 fusion.19
  10.3 0.0 copy-start.3
  10.3 16.6 %gather_fusion = bf16[1024,2048]{1,0:T(8,128)(2,1)} fusion(bf16[4000,2048]{1,0:T(8,128)(2,1)} %param.13, s32[1024]{0:T(1024)S(1)} %fusion.19), kind=kCustom, calls=%fused_computation | custom fusion | bytes 8392704 | tf_op jit(solution)/shard_map/jit(_take)/gather | solution.py:459
  26.9 0.0 copy-done.3
  26.9 4.1 %select_select_fusion = bf16[1024,2048]{1,0:T(8,128)(2,1)} fusion(bf16[1024,2048]{1,0:T(8,128)(2,1)} %gather_fusion, pred[1024]{0:T(1024)(128)(4,1)S(1)} %get-tuple-element.28, pred[1024]{0:T(1024)(128)(4,1)S(1)} %get-tuple-element.27), kind=kLoop, calls=%fused_computation.18 | loop fusion | flops 4194304 | bytes 8390656 | tf_op jit(solution)/shard_map/jit(_where)/select_n | solution.py:460
  31.0 0.0 reduce-scatter.3.cloned.1.call-update
  31.0 0.0 copy-start.6
  31.0 0.0 copy-start.1
  31.0 0.6 reduce-scatter.5.cloned.1.call-start
  31.6 35.0 %fusion.7 = bf16[1024,5632]{1,0:T(8,128)(2,1)} fusion(bf16[1,2048,5632]{2,1,0:T(8,128)(2,1)} %param.16, bf16[1,1024,2048]{2,1,0:T(8,128)(2,1)} %param.15), kind=kOutput, calls=%fused_computation.9 | convolution fusion | flops 23674224640 | bytes 38797312 | tf_op jit(solution)/shard_map/dot_general | solution.py:456
  66.6 0.0 copy-done.6
  66.6 0.0 copy-done.1
  66.6 0.1 convert_reduce_fusion
  66.7 0.0 copy-start.7
  66.7 0.5 copy-done.7
  67.2 0.1 convert_divide_fusion
  67.3 0.6 pad_maximum_fusion.1.rows_ref
  67.9 0.0 all-gather.3.cloned.1.call-done
  67.9 173.1 %head.1 = (bf16[2048,4000]{1,0:T(8,128)(2,1)}, bf16[2048,2048]{1,0:T(8,128)(2,1)}, f32[128,2048]{1,0:T(8,128)}, f32[4,128,2048]{2,1,0:T(8,128)}, f32[4,128,2048]...) custom-call(bf16[1024,2048]{1,0:T(8,128)(2,1)} %bitcast.28, ...), custom_call_target="tpu_custom_call" | custom-call | flops 67108864000 | bytes 80000000 | tf_op jit(solution)/shard_map/head/pallas_call | solution.py:417
  241.0 0.0 reduce-scatter.3.cloned.1.call-done
  241.1 0.0 reduce-scatter.5.cloned.1.call-update
  241.1 0.0 copy-start.2
  241.1 0.0 copy-start.4
  241.1 0.0 copy-start.5
  241.1 0.0 copy-start.8
  241.1 0.0 copy-start.9
  241.1 32.1 %fusion.14 = bf16[1,1024,2048]{2,1,0:T(8,128)(2,1)} fusion(bf16[1,1024,2048]{2,1,0:T(8,128)(2,1)} %param.15, bf16[1024,5632]{1,0:T(8,128)(2,1)} %fusion.7, bf16[1,5632,2048]{2,1,0:T(8,128)(2,1)} %param.17), kind=kOutput, calls=%fused_computation.16 | convolution fusion | flops 23628611584 | bytes 42991616 | tf_op jit(solution)/shard_map/dot_general | solution.py:471
  273.3 0.0 copy-done.2
  273.3 0.0 copy-done.4
  273.3 0.0 copy-done.5
  273.3 0.1 fusion.18
  273.4 0.0 copy-done.8
  273.4 0.5 fusion.20
  273.9 0.0 copy-done.9
  273.9 0.0 copy-start
  273.9 41.2 %convolution_convert_fusion = bf16[4000,2048]{1,0:T(8,128)(2,1)} fusion(bf16[2048,4000]{1,0:T(8,128)(2,1)S(1)} %copy-done.9, bf16[2048,2048]{1,0:T(8,128)(2,1)} %get-tuple-element.22), kind=kOutput, calls=%fused_computation.14 | convolution fusion | flops 33562624000 | bytes 41156608 | tf_op jit(solution)/shard_map/dot_general | solution.py:470
  315.2 3.6 %reduce-scatter.5.cloned.1.call-done = f32[1,128,2048]{2,1,0:T(8,128)} async-done(((f32[4,128,2048]{2,1,0:T(8,128)}), f32[1,128,2048]{2,1,0:T(8,128)}) %reduce-scatter.5.cloned.1.call-update) | async-done | bytes 1048592 | tf_op jit(solution)/shard_map/reduce_scatter | solution.py:468
  318.8 0.0 copy-done
  318.8 2.7 pad_maximum_fusion
  (5 shorter events, 0.0 us)
Async XLA Ops:
  7.2 60.8 %all-gather.3.cloned.1.call-start = ((), (), s32[]{:S(2)}) async-start(), calls=%async_computation.4 | async-start | bytes 4718592 | tf_op jit(solution)/shard_map/all_gather | solution.py:450
  9.5 231.5 %reduce-scatter.3.cloned.1.call-start = ((), (), s32[]{:S(2)}) async-start(), calls=%async_computation.2 | async-start | bytes 4718592 | tf_op jit(solution)/shard_map/reduce_scatter | solution.py:462
  10.3 16.6 %copy-start.3 = (s32[1024]{0:T(1024)S(1)}, s32[1024]{0:T(1024)}, u32[]{:S(2)}) copy-start(s32[1024]{0:T(1024)} %param.14) | copy-start | bytes 12292
  31.0 35.6 %copy-start.6 = (s32[2,1024]{1,0:T(2,128)S(1)}, s32[2,1024]{1,0:T(2,128)}, u32[]{:S(2)}) copy-start(s32[2,1024]{1,0:T(2,128)} %param.11) | copy-start | bytes 24580
  31.0 35.6 %copy-start.1 = (s32[2,1024]{1,0:T(2,128)S(1)}, s32[2,1024]{1,0:T(2,128)}, u32[]{:S(2)}) copy-start(s32[2,1024]{1,0:T(2,128)} %param.12) | copy-start | bytes 24580
  31.0 287.8 %reduce-scatter.5.cloned.1.call-start = ((), (), s32[]{:S(2)}) async-start(), calls=%async_computation.3 | async-start | bytes 5242880 | tf_op jit(solution)/shard_map/reduce_scatter | solution.py:468
  66.7 0.5 copy-start.7
  241.1 32.2 %copy-start.2 = (s32[2,1024]{1,0:T(2,128)S(1)}, s32[2,1024]{1,0:T(2,128)}, u32[]{:S(2)}) copy-start(s32[2,1024]{1,0:T(2,128)} %param.12) | copy-start | bytes 24580
  241.1 32.2 %copy-start.4 = (f32[2,1,1024]{2,1,0:T(1,128)S(1)}, f32[2,1,1024]{2,1,0:T(1,128)}, u32[]{:S(2)}) copy-start(f32[2,1,1024]{2,1,0:T(1,128)} %get-tuple-element.16) | copy-start | bytes 24580
  241.1 32.2 %copy-start.5 = (f32[2,1,1024]{2,1,0:T(1,128)S(1)}, f32[2,1,1024]{2,1,0:T(1,128)}, u32[]{:S(2)}) copy-start(f32[2,1,1024]{2,1,0:T(1,128)} %get-tuple-element.17) | copy-start | bytes 24580
  241.1 32.3 %copy-start.8 = (f32[2]{0:T(128)S(1)}, f32[2]{0:T(128)}, u32[]{:S(2)}) copy-start(f32[2]{0:T(128)} %copy-done.7) | copy-start | bytes 28
  241.1 32.8 %copy-start.9 = (bf16[2048,4000]{1,0:T(8,128)(2,1)S(1)}, bf16[2048,4000]{1,0:T(8,128)(2,1)}, u32[]{:S(2)}) copy-start(bf16[2048,4000]{1,0:T(8,128)(2,1)} %get-tuple-element.21) | copy-start | bytes 49152004
  273.9 44.9 %copy-start = (f32[128,2048]{1,0:T(8,128)S(1)}, f32[128,2048]{1,0:T(8,128)}, u32[]{:S(2)}) copy-start(f32[128,2048]{1,0:T(8,128)} %get-tuple-element.18) | copy-start | bytes 3145732
Sparse Core Ops, SparseCore 0:
  9.6 49.2 all-gather.2
  61.8 72.3 reduce-scatter.2
  241.2 77.5 reduce-scatter.4

commit v2 on v1

--- a/solution.py
+++ b/solution.py
@@ -20,10 +20,11 @@
     return lax.dot_general(a, b, (((1,), (1,)), ((), ())), preferred_element_type=F32)
 
 
-def head_kernel(n, tile, chunk, x0_hbm, hid_ref, rows_ref, w_hbm, g_hbm, xall, dx0_hbm, dx1_hbm, prx, prx1, rx, lse_ref, tgt_ref,
-                w, z, xbuf, cols, g_buf, blk, dxb, stage, mine, peers,
+def head_kernel(n, tile, chunk, x0_hbm, hid_ref, rows_ref, w_hbm, emb_hbm, g_hbm, xall, dx0_hbm, dx1_hbm, h0_hbm, prx, prx1, rx, hp, hrx, lse_ref, tgt_ref,
+                w, z, xbuf, cols, g_buf, blk, dxb, stage, mine, peers, hb, hst,
                 w_sem, x_sem, xs_sem, own_sem, ag_send, ag_recv, st_send, st_recv, g_sem,
-                pr_send, pr_recv, pr1_send, pr1_recv, rs_send, rs_recv, stage_sem, out_sem, out1_sem):
+                pr_send, pr_recv, pr1_send, pr1_recv, rs_send, rs_recv, stage_sem, out_sem, out1_sem,
+                hp_send, hp_recv, hx_send, hx_recv, hl_sem, hs_sem, ho_sem):
     me = lax.axis_index("stage")
     zc, c = me // 2, me % 2
     inner_to_outer = 3 * zc - 3
@@ -152,26 +153,55 @@
     def rs_copy(s, k, tz):
         return remote(blk.at[s, own_half], rx.at[k], rs_send.at[k], rs_recv.at[k], tz, c)
 
-    def combine(s, slots):
-        pair_copy(s).wait_recv()
-        stages = [pltpu.make_async_copy(prx.at[s], stage.at[0], stage_sem.at[0])]
-        stages[0].start()
-        for q, k in enumerate(slots):
-            rs_copy(s, k, zc).wait_recv()
-            copy = pltpu.make_async_copy(rx.at[k], stage.at[1 + q], stage_sem.at[1 + q])
-            copy.start()
-            stages.append(copy)
-        for copy in stages:
-            copy.wait()
+    def stage_add(into, src):
+        copy = pltpu.make_async_copy(src, stage, stage_sem)
+        copy.start()
+        copy.wait()
 
         @pl.loop(0, half // 16)
         def _(r):
             here = pl.ds(pl.multiple_of(c * half + r * 16, 16), 16)
-            there = pl.ds(pl.multiple_of(r * 16, 16), 16)
-            total = blk[s, here, :] + stage[0, there, :]
-            for q in range(len(slots)):
-                total = total + stage[1 + q, there, :]
-            blk[s, here, :] = total
+            into[here, :] = into[here, :] + stage[pl.ds(pl.multiple_of(r * 16, 16), 16), :]
+
+    def combine(s, slots):
+        pair_copy(s).wait_recv()
+        stage_add(blk.at[s], prx.at[s])
+        for k in slots:
+            rs_copy(s, k, zc).wait_recv()
+            stage_add(blk.at[s], rx.at[k])
+
+    far = zc // 2
+    order = [3 - 3 * far, 2 - far, zc + 1 - 2 * (zc % 2), zc]
+
+    def h_rows(s, core):
+        return emb_hbm.at[pl.ds(pl.multiple_of(order[s] * tile + core * half, half), half)]
+
+    def h_load(s):
+        return pltpu.make_async_copy(h_rows(s, c), hb.at[s], hl_sem.at[s])
+
+    def h_pair(s):
+        return remote(h_rows(s, 1 - c), hp.at[s], hp_send.at[s], hp_recv.at[s], zc, 1 - c)
+
+    def h_copy(s, k, tz):
+        return remote(hb.at[s], hrx.at[k], hx_send.at[k], hx_recv.at[k], tz, c)
+
+    def h_add(s, src, sem):
+        copy = pltpu.make_async_copy(src, hst, sem)
+        copy.start()
+        copy.wait()
+
+        @pl.loop(0, half // 16)
+        def _(r):
+            here = pl.ds(pl.multiple_of(r * 16, 16), 16)
+            hb[s, here, :] = hb[s, here, :] + hst[here, :]
+
+    def h_combine(s, slots):
+        h_load(s).wait()
+        h_pair(s).wait_recv()
+        h_add(s, hp.at[s], hs_sem)
+        for k in slots:
+            h_copy(s, k, zc).wait_recv()
+            h_add(s, hrx.at[k], hs_sem)
 
     set_cols(0, None)
     pl.semaphore_wait(barrier, n - 1)
@@ -207,6 +237,10 @@
         block = lax.rem(zc + k, 4)
         return ag(xrows(block, c), block, 5 + k, 3 + k, zc, 1 - c, c)
 
+    for s in range(steps):
+        h_load(s).start()
+        h_pair(s).start()
+
     @pl.when(is_outer)
     def _():
         hop_outer().start()
@@ -220,6 +254,11 @@
     x_load(0, 1, 1).start()
     x_store(0, 0).start()
     logits_tile(0, 0, 0, True)
+
+    @pl.when(is_outer)
+    def _():
+        h_combine(0, [])
+        h_copy(0, 0, outer_to_inner).start()
 
     @pl.loop(1, steps)
     def _(i):
@@ -241,6 +280,11 @@
             got(other_inner, 2, c)
             hop_inner(3).start()
 
+        @pl.when((i == 1) & is_outer)
+        def _():
+            h_combine(1, [])
+            h_copy(1, 1, outer_to_inner).start()
+
     x_store(steps - 1, (steps - 1) % 2).wait()
     stat_send(0)
 
@@ -248,13 +292,19 @@
     def _():
         got(other_outer, 3, c)
         hop_inner(4).start()
+        h_combine(0, [0])
+        h_copy(0, 3, other_inner).start()
+
+    @pl.when(is_outer)
+    def _():
+        h_combine(2, [])
+        h_copy(2, 2, outer_to_inner).start()
 
     stat_finish(0)
 
     @pl.loop(0, steps)
     def _(s):
         slot = lax.rem(s, 2)
-        far = zc // 2
         pick = jnp.where(s == 0, 3 - 3 * far, jnp.where(s == 1, 2 - far, jnp.where(s == 2, zc + 1 - 2 * (zc % 2), zc)))
         at = pl.multiple_of(pick * tile, tile)
 
@@ -270,6 +320,13 @@
         def _():
             combine(0, [])
             rs_copy(0, 0, outer_to_inner).start()
+
+        @pl.when((s == 1) & is_inner)
+        def _():
+            h_combine(1, [1])
+            h_copy(1, 4, other_inner).start()
+            h_combine(2, [3])
+            h_copy(2, 5, inner_to_outer).start()
 
         @pl.when(s == 2)
         def _():
@@ -314,11 +371,18 @@
 
     stat_send(1)
 
+    @pl.when(is_inner)
+    def _():
+        h_combine(3, [2, 4])
+
     @pl.when(is_outer)
     def _():
         combine(2, [])
         rs_copy(2, 2, outer_to_inner).start()
-
+        h_combine(3, [5])
+
+    h_out = pltpu.make_async_copy(hb.at[3], h0_hbm, ho_sem)
+    h_out.start()
     stat_finish(1)
 
     def pair1(i, slot):
@@ -329,15 +393,7 @@
 
     def finish1(i, slot):
         pair1(i, slot).wait_recv()
-        copy = pltpu.make_async_copy(prx1.at[i], stage.at[0], stage_sem.at[0])
-        copy.start()
-        copy.wait()
-
-        @pl.loop(0, half // 16)
-        def _(r):
-            here = pl.ds(pl.multiple_of(c * half + r * 16, 16), 16)
-            dxb[slot, here, :] = dxb[slot, here, :] + stage[0, pl.ds(pl.multiple_of(r * 16, 16), 16), :]
-
+        stage_add(dxb.at[slot], prx1.at[i])
         out1(i, slot).start()
 
     @pl.loop(0, steps)
@@ -386,12 +442,15 @@
         forward(k).wait_send()
     for s in range(steps):
         pair_copy(s).wait_send()
+        h_pair(s).wait_send()
+    h_out.wait()
 
     @pl.when(is_outer)
     def _():
         hop_outer().wait_send()
         for k in range(3):
             rs_copy(k, k, outer_to_inner).wait_send()
+            h_copy(k, k, outer_to_inner).wait_send()
 
     @pl.when(is_inner)
     def _():
@@ -400,11 +459,14 @@
         rs_copy(0, 3, other_inner).wait_send()
         rs_copy(1, 4, other_inner).wait_send()
         rs_copy(2, 5, inner_to_outer).wait_send()
+        h_copy(0, 3, other_inner).wait_send()
+        h_copy(1, 4, other_inner).wait_send()
+        h_copy(2, 5, inner_to_outer).wait_send()
 
     final.wait()
 
 
-def head(x0, hid1, rows_in, w, n, tile=256, chunk=1024):
+def head(x0, hid1, rows_in, w, emb, n, tile=256, chunk=1024):
     tokens, width = x0.shape
     rows = w.shape[0]
     half = tile // 2
@@ -417,10 +479,11 @@
     return pl.pallas_call(
         functools.partial(head_kernel, n, tile, chunk),
         out_shape=(sds((2 * tokens, rows), BF16), sds((2 * tokens, width), BF16), sds((half, width), F32),
-                   sds((steps, half, width), F32), sds((steps, half, width), F32), sds((steps, half, width), F32),
-                   sds((6, half, width), F32), sds((2, 1, tokens), F32), sds((2, 1, tokens), F32)),
-        in_specs=[hbm, vmem, vmem, hbm],
-        out_specs=(hbm, hbm, hbm, hbm, hbm, hbm, hbm, vmem, vmem),
+                   sds((steps, half, width), F32), sds((half, width), BF16), sds((steps, half, width), F32),
+                   sds((steps, half, width), F32), sds((6, half, width), F32), sds((steps, half, width), BF16),
+                   sds((6, half, width), BF16), sds((2, 1, tokens), F32), sds((2, 1, tokens), F32)),
+        in_specs=[hbm, vmem, vmem, hbm, hbm],
+        out_specs=(hbm,) * 10 + (vmem, vmem),
         scratch_shapes=[
             pltpu.VMEM((rows, width), BF16),
             pltpu.VMEM((tokens, rows), F32),
@@ -429,17 +492,20 @@
             pltpu.VMEM((2, tile, rows), BF16),
             pltpu.VMEM((steps, tile, width), F32),
             pltpu.VMEM((2, tile, width), F32),
-            pltpu.VMEM((3, half, width), F32),
+            pltpu.VMEM((half, width), F32),
             pltpu.VMEM((2, 8, tokens), F32),
             pltpu.VMEM((2, n, 8, tokens), F32),
+            pltpu.VMEM((steps, half, width), BF16),
+            pltpu.VMEM((half, width), BF16),
             dma((nchunk,)), dma((2,)), dma((2,)), dma,
             dma((9,)), dma((7,)), dma((2, n)), dma((2, n)), dma((2,)),
-            dma((steps,)), dma((steps,)), dma((2,)), dma((steps,)), dma((6,)), dma((6,)), dma((3,)), dma, dma((2,)),
+            dma((steps,)), dma((steps,)), dma((2,)), dma((steps,)), dma((6,)), dma((6,)), dma, dma, dma((2,)),
+            dma((steps,)), dma((steps,)), dma((6,)), dma((6,)), dma((steps,)), dma, dma,
         ],
         compiler_params=pltpu.CompilerParams(collective_id=0, has_side_effects=True, vmem_limit_bytes=67043328),
         cost_estimate=pl.CostEstimate(flops=8 * tokens * rows * width, bytes_accessed=80_000_000, transcendentals=4 * tokens * rows),
         name="head",
-    )(x0, hid1, rows_in, w)
+    )(x0, hid1, rows_in, w, emb)
 
 
 def stage_body(hidden, w_head, labels, loss_mask, w_embed, tok_ids, act_in, w_up, w_down):
@@ -459,12 +525,10 @@
     own_rows = jnp.take(w_embed, jnp.clip(id_off, 0, shard_rows - 1), axis=0)
     own_rows = jnp.where(inside[:, None], own_rows, jnp.zeros_like(own_rows))
 
-    embedded = lax.psum_scatter(own_rows, "stage", scatter_dimension=0, tiled=True)
     inner, own_rows, x0 = lax.optimization_barrier((inner, own_rows, x0))
 
     rows_in = jnp.stack([(labels - start).astype(F32), tok_scale], axis=1)
-    g, x_all, dx0, dx1, _, _, _, lse, target = head(x0, hidden[1], rows_in, w_head, n)
-    dx1, embedded = lax.optimization_barrier((dx1, embedded))
+    g, x_all, dx0, dx1, embedded, _, _, _, _, _, lse, target = head(x0, hidden[1], rows_in, w_head, own_rows, n)
     dx1 = lax.psum_scatter(dx1, "stage", scatter_dimension=0, tiled=False, axis_index_groups=[[0, 2, 4, 6], [1, 3, 5, 7]])
     micro_loss = jnp.sum(weights * (lse[:, 0] - target[:, 0]), axis=1) / kept_count
     grad_head = lax.dot_general(g, x_all, (((0,), (0,)), ((), ())), preferred_element_type=F32).astype(BF16)

time: 332 us -> 321 us (0.967)
  Pallas kernels: 173 us -> 157 us
    pallas_call x1, Pallas kernels: 173 us -> 157 us  [head(): pl.pallas_call(functools.partial(head_kernel, n, tile, chunk), out_shape=...]
  transfers between devices with their start and end apart: 3 -> 2, of which waited for: 1 -> 1; matrix products, arithmetic and copies ran while one was open for 40% -> 42% of each run, Pallas kernels for 53% -> 0%
where the time goes in v2:
time: 321 us; the launch traced here: 317 us
  Pallas kernels  157 us (49%)
  matrix products  108 us (34%)
  local copies, waits for them, and re-layouts  20.7 us (6%)
  between operations  14.4 us (4%)
  other arithmetic  11.1 us (3%)
  waiting for transfers between devices  6.03 us (2%)
    pallas_call x1, Pallas kernels, head(): pl.pallas_call(functools.partial(head_kernel, n, tile, chunk), out_shape=...  157 us
    dot_general x1, matrix products, stage_body(): lax.dot_general(g, x_all, (((0,), (0,)), ((), ())), preferred_element_typ...  41.2 us
    dot_general x1, matrix products, stage_body(): jnp.dot(layer_in, w_up[0], preferred_element_type=F32)  34.9 us
    dot_general x1, matrix products, stage_body(): jnp.dot(inner, w_down[0], preferred_element_type=F32)  31.9 us
    gather x1, local copies, waits for them, and re-layouts, stage_body(): own_rows = jnp.take(w_embed, jnp.clip(id_off, 0, shard_rows - 1), axis=0)  17.1 us
  transfers between devices with their start and end apart: 2, of which 1 were waited for; matrix products, arithmetic and copies ran while one was open for 42% of the time, Pallas kernels for 0%

profile of v2, /device:TPU:0, one launch (start us, length us, event | category | flops | bytes accessed | tf_op | source)
XLA Modules:
  0.0 317.3 jit_solution(1734091998998705296)
XLA Ops:
  7.2 0.0 all-gather.3.cloned.1.call-start
  7.2 2.3 slice_bitcast_fusion
  9.5 0.0 all-gather.3.cloned.1.call-update
  9.5 0.0 reduce-scatter.2.cloned.1.call-start
  9.6 0.7 subtract_convert_fusion
  10.3 0.8 convert_reduce_fusion
  11.1 0.0 copy-start.6
  11.1 0.5 copy-done.6
  11.6 0.8 convert_divide_fusion
  12.4 0.7 fusion.19
  13.1 0.0 copy-start.3
  13.1 17.1 %gather_fusion = bf16[1024,2048]{1,0:T(8,128)(2,1)} fusion(bf16[4000,2048]{1,0:T(8,128)(2,1)} %param.13, s32[1024]{0:T(1024)S(1)} %fusion.19), kind=kCustom, calls=%fused_computation | custom fusion | bytes 8392704 | tf_op jit(solution)/shard_map/jit(_take)/gather | solution.py:525
  30.2 0.6 pad_maximum_fusion.1.rows_ref
  30.8 0.0 copy-done.3
  30.8 4.1 %select_select_fusion.emb_hbm = bf16[1024,2048]{1,0:T(8,128)(2,1)} fusion(bf16[1024,2048]{1,0:T(8,128)(2,1)} %gather_fusion, pred[1024]{0:T(1024)(128)(4,1)S(1)} %get-tuple-element.28, pred[1024]{0:T(1024)(128)(4,1)S(1)} %get-tuple-element.27), kind=kLoop, calls=%fused_computation.18 | loop fusion | flops 4194304 | bytes 8390656 | tf_op jit(solution)/shard_map/jit(_where)/select_n | solution.py:526
  34.9 34.9 %fusion.7 = bf16[1024,5632]{1,0:T(8,128)(2,1)} fusion(bf16[1,2048,5632]{2,1,0:T(8,128)(2,1)} %param.16, bf16[1,1024,2048]{2,1,0:T(8,128)(2,1)} %param.15), kind=kOutput, calls=%fused_computation.9 | convolution fusion | flops 23674224640 | bytes 38797312 | tf_op jit(solution)/shard_map/dot_general | solution.py:522
  69.8 0.0 all-gather.3.cloned.1.call-done
  69.8 156.9 %head.1 = (bf16[2048,4000]{1,0:T(8,128)(2,1)}, bf16[2048,2048]{1,0:T(8,128)(2,1)}, f32[128,2048]{1,0:T(8,128)}, f32[4,128,2048]{2,1,0:T(8,128)}, bf16[128,2048]{...) custom-call(bf16[1024,2048]{1,0:T(8,128)(2,1)} %bitcast.28, ...), custom_call_target="tpu_custom_call" | custom-call | flops 67108864000 | bytes 80000000 | tf_op jit(solution)/shard_map/head/pallas_call | solution.py:479
  226.8 0.0 reduce-scatter.2.cloned.1.call-update
  226.8 0.0 copy-start.2
  226.8 0.0 copy-start.4
  226.8 0.0 copy-start.5
  226.8 0.0 copy-start.7
  226.9 0.0 copy-start.8
  226.9 31.9 %fusion.14 = bf16[1,1024,2048]{2,1,0:T(8,128)(2,1)} fusion(bf16[1,1024,2048]{2,1,0:T(8,128)(2,1)} %param.15, bf16[1024,5632]{1,0:T(8,128)(2,1)} %fusion.7, bf16[1,5632,2048]{2,1,0:T(8,128)(2,1)} %param.17), kind=kOutput, calls=%fused_computation.16 | convolution fusion | flops 23628611584 | bytes 42991616 | tf_op jit(solution)/shard_map/dot_general | solution.py:535
  258.7 0.0 copy-done.2
  258.7 0.0 copy-done.4
  258.8 0.0 copy-done.5
  258.8 0.1 fusion.18
  258.9 0.0 copy-done.7
  258.9 0.5 fusion.20
  259.4 0.0 copy-done.8
  259.4 0.0 copy-start
  259.4 0.0 copy-start.1
  259.4 41.2 %convolution_convert_fusion = bf16[4000,2048]{1,0:T(8,128)(2,1)} fusion(bf16[2048,4000]{1,0:T(8,128)(2,1)S(1)} %copy-done.8, bf16[2048,2048]{1,0:T(8,128)(2,1)} %get-tuple-element.22), kind=kOutput, calls=%fused_computation.14 | convolution fusion | flops 33562624000 | bytes 41156608 | tf_op jit(solution)/shard_map/dot_general | solution.py:534
  300.7 6.0 %reduce-scatter.2.cloned.1.call-done = f32[1,128,2048]{2,1,0:T(8,128)} async-done(((f32[4,128,2048]{2,1,0:T(8,128)}), f32[1,128,2048]{2,1,0:T(8,128)}) %reduce-scatter.2.cloned.1.call-update) | async-done | bytes 1048592 | tf_op jit(solution)/shard_map/reduce_scatter | solution.py:532
  306.7 0.0 copy-done
  306.7 2.7 pad_maximum_fusion
  309.4 0.0 copy-done.1
  309.4 0.8 copy.21
  (4 shorter events, 0.0 us)
Async XLA Ops:
  7.2 62.7 %all-gather.3.cloned.1.call-start = ((), (), s32[]{:S(2)}) async-start(), calls=%async_computation.2 | async-start | bytes 4718592 | tf_op jit(solution)/shard_map/all_gather | solution.py:516
  9.5 297.2 %reduce-scatter.2.cloned.1.call-start = ((), (), s32[]{:S(2)}) async-start(), calls=%async_computation.1 | async-start | bytes 5242880 | tf_op jit(solution)/shard_map/reduce_scatter | solution.py:532
  11.1 0.5 copy-start.6
  13.1 17.7 %copy-start.3 = (s32[1024]{0:T(1024)S(1)}, s32[1024]{0:T(1024)}, u32[]{:S(2)}) copy-start(s32[1024]{0:T(1024)} %param.14) | copy-start | bytes 12292
  226.8 31.9 %copy-start.2 = (s32[2,1024]{1,0:T(2,128)S(1)}, s32[2,1024]{1,0:T(2,128)}, u32[]{:S(2)}) copy-start(s32[2,1024]{1,0:T(2,128)} %param.12) | copy-start | bytes 24580
  226.8 31.9 %copy-start.4 = (f32[2,1,1024]{2,1,0:T(1,128)S(1)}, f32[2,1,1024]{2,1,0:T(1,128)}, u32[]{:S(2)}) copy-start(f32[2,1,1024]{2,1,0:T(1,128)} %get-tuple-element.17) | copy-start | bytes 24580
  226.8 31.9 %copy-start.5 = (f32[2,1,1024]{2,1,0:T(1,128)S(1)}, f32[2,1,1024]{2,1,0:T(1,128)}, u32[]{:S(2)}) copy-start(f32[2,1,1024]{2,1,0:T(1,128)} %get-tuple-element.18) | copy-start | bytes 24580
  226.8 32.1 %copy-start.7 = (f32[2]{0:T(128)S(1)}, f32[2]{0:T(128)}, u32[]{:S(2)}) copy-start(f32[2]{0:T(128)} %copy-done.6) | copy-start | bytes 28
  226.9 32.6 %copy-start.8 = (bf16[2048,4000]{1,0:T(8,128)(2,1)S(1)}, bf16[2048,4000]{1,0:T(8,128)(2,1)}, u32[]{:S(2)}) copy-start(bf16[2048,4000]{1,0:T(8,128)(2,1)} %get-tuple-element.21) | copy-start | bytes 49152004
  259.4 47.3 %copy-start = (f32[128,2048]{1,0:T(8,128)S(1)}, f32[128,2048]{1,0:T(8,128)}, u32[]{:S(2)}) copy-start(f32[128,2048]{1,0:T(8,128)} %get-tuple-element.19) | copy-start | bytes 3145732
  259.4 50.0 %copy-start.1 = (bf16[128,2048]{1,0:T(8,128)(2,1)S(1)}, bf16[128,2048]{1,0:T(8,128)(2,1)}, u32[]{:S(2)}) copy-start(bf16[128,2048]{1,0:T(8,128)(2,1)} %get-tuple-element.37) | copy-start | bytes 1572868
Sparse Core Ops, SparseCore 0:
  10.1 49.2 all-gather.2
  226.9 79.6 reduce-scatter.1
